TPU v7x, 256 devices: a 8x8x2 block of a 8x8x16 slice. The times are simulated.
256 devices in a mesh: grp: 2 (over z), kv: 128 (over y, x, core).
Axes of the slice: x: 8, y: 8, z: 2, core: 2. Of those that a mesh axis runs over, the one named last changes fastest.
The devices are a block of a 8x8x16 slice.
Arguments:
- queries: bfloat16 [1024, 40, 128], P(('grp', 'kv')), parts along dimension 0, may hold values from -250 to 250
- cache_keys: bfloat16 [65536, 40, 128], P(('grp', 'kv')), parts along dimension 0, may hold values from -8 to 8
- cache_values: bfloat16 [65536, 40, 128], P(('grp', 'kv')), parts along dimension 0, may hold values from -18 to 18
- new_keys: bfloat16 [1024, 40, 128], P(('grp', 'kv')), parts along dimension 0, may hold values from -4 to 4
- new_values: bfloat16 [1024, 40, 128], P(('grp', 'kv')), parts along dimension 0, may hold values from -4 to 4
- valid_frames: int32 [2], P('grp'), parts along dimension 0, may hold values from 64 to 128
Outputs:
- attended: bfloat16 [1024, 40, 128], P(('grp', 'kv')), parts along dimension 0
There are 2 independent parts, one for each index of `grp`. A program takes and returns all parts, laid end to end along the dimension named above; each array names one. Nothing has to cross between parts.
All inputs are finite; a program needn't handle non-finite values.
Results may differ from a plain program's by a relative error of at most 0.0027.
Values may be sent and summed in bfloat16 or wider, within the bound.
A program may use at most 128 MiB of HBM per device.

v0:
```python
import functools
import math
import jax
import jax.numpy as jnp
from jax import lax
from jax.sharding import Mesh
from jax.sharding import PartitionSpec as P

FRAME = 256
QUERY_SPLIT = 4
KV = ("kv_0", "kv_1", "kv_2")
GRP_KV = ("grp", "kv_0", "kv_1", "kv_2")
masked_score = -1e30


def by_axis(x, axes):
    return functools.reduce(lax.pmax, axes, x)


def split_up(x, dim, peers):
    before, after = (x.shape[:dim], x.shape[dim + 1 :])
    return jnp.moveaxis(x.reshape(*before, peers, -1, *after), dim, 0)


def sum_packed(arrays, axis, dims):
    peers = lax.axis_size(axis)
    parts = [split_up(a, dim, peers) for a, dim in zip(arrays, dims)]
    lines = jnp.concatenate([b.reshape(peers, -1) for b in parts], axis=1)
    extent = max(16, -(-lines.shape[1] // 1024) * 8)
    lines = jnp.pad(lines, ((0, 0), (0, extent * 128 - lines.shape[1]))).reshape(-1, 128)
    line, at, done = (lax.psum_scatter(lines, axis, tiled=True).reshape(-1), 0, [])
    for b in parts:
        part = b[0]
        done.append(line[at : at + part.size].reshape(part.shape))
        at += part.size
    return tuple(done)


def per_device(queries, cache_keys, cache_values, new_keys, new_values, valid_frames):
    q_dev, heads, head_dim = queries.shape
    cache_dev = cache_keys.shape[0]
    factor = 1.0 / math.sqrt(head_dim)
    gathered = lax.all_gather(queries, KV, axis=0, tiled=True)
    devices = lax.axis_size(KV)
    position = lax.axis_index(KV) * cache_dev + lax.iota(jnp.int32, cache_dev)
    live = position < valid_frames[0] * FRAME
    per_block = q_dev // QUERY_SPLIT
    blocked = gathered.reshape(devices, QUERY_SPLIT, per_block, heads, head_dim)
    pieces = []
    half = heads // 2
    for index in range(QUERY_SPLIT):
        block = blocked[:, index].reshape(devices * per_block, heads, head_dim)
        halves = []
        for which in range(2):
            lower = which * half
            sub_block = block[:, lower : lower + half]
            ckeys = cache_keys[:, lower : lower + half]
            nkeys = new_keys[:, lower : lower + half]
            block_cache_score = (
                jnp.einsum("qhd,khd->hqk", sub_block, ckeys, preferred_element_type=jnp.float32)
                * factor
            )
            block_cache_score = jnp.where(
                live[None, None, :], block_cache_score, jnp.float32(masked_score)
            )
            block_new_score = (
                jnp.einsum("qhd,khd->hqk", sub_block, nkeys, preferred_element_type=jnp.float32)
                * factor
            )
            top = by_axis(
                jnp.maximum(jnp.max(block_cache_score, axis=2), jnp.max(block_new_score, axis=2)),
                KV,
            )
            cache_weight = jnp.exp(block_cache_score - top[:, :, None])
            new_weight = jnp.exp(block_new_score - top[:, :, None])
            total = jnp.sum(cache_weight, axis=2) + jnp.sum(new_weight, axis=2)
            numerator = jnp.einsum(
                "hqk,khd->qhd",
                cache_weight.astype(jnp.bfloat16),
                cache_values[:, lower : lower + half],
                preferred_element_type=jnp.float32,
            )
            numerator = numerator + jnp.einsum(
                "hqk,khd->qhd",
                new_weight.astype(jnp.bfloat16),
                new_values[:, lower : lower + half],
                preferred_element_type=jnp.float32,
            )
            numerator, total = (numerator, total.T)
            summed, denominator = sum_packed((numerator, total), KV, (0, 0))
            halves.append((summed / denominator[:, :, None]).astype(jnp.bfloat16))
        pieces.append(jnp.concatenate(halves, axis=1))
    return jnp.concatenate(pieces, axis=0)


def solution(mesh):
    torus = Mesh(mesh.devices.reshape(mesh.shape["grp"], 8, 8, 2), ("grp", "kv_0", "kv_1", "kv_2"))
    return jax.shard_map(
        per_device,
        mesh=torus,
        in_specs=(
            P(GRP_KV, None, None),
            P(GRP_KV, None, None),
            P(GRP_KV, None, None),
            P(GRP_KV, None, None),
            P(GRP_KV, None, None),
            P("grp"),
        ),
        out_specs=P(GRP_KV, None, None),
        check_vma=False,
    )
```

profile of v0, /device:TPU:518, one launch (start us, length us, event | category | flops | bytes accessed | tf_op | source)
XLA Modules:
  0.0 733.7 jit_solution(5114170117710780032)
XLA Ops:
  8.0 4.3 fusion.169
  17.2 4.3 fusion.170
  21.5 87.6 %all-gather.2.cloned.1.call-done = bf16[512,40,128]{2,1,0:T(8,128)(2,1)} async-done(((bf16[4,40,128]{2,1,0:T(8,128)(2,1)}), bf16[512,40,128]{2,1,0:T(8,128)(2,1)}) %all-gather.2.cloned.1.call-update) | async-done | bytes 5242896 | tf_op jit(solution)/shard_map/all_gather | solution.py:43
  109.1 3.6 fusion.168
  131.8 28.8 %pmax.168 = f32[20,128]{1,0:T(8,128)S(1)} all-reduce(f32[20,128]{1,0:T(8,128)S(1)} %max.72), channel_id=1, replica_groups=mesh['grp'=2,'kv_0'=8,'kv_1'=8,'kv_2'=2] {'kv_0'}, use_global_device_ids=true, to_apply=%region_2.3 | all-reduce | flops 2560 | bytes 20480 | tf_op jit(solution)/shard_map/pmax | solution.py:17
  160.6 26.6 %pmax.169 = f32[20,128]{1,0:T(8,128)S(1)} all-reduce(f32[20,128]{1,0:T(8,128)S(1)} %pmax.168), channel_id=1, replica_groups=mesh['grp'=2,'kv_0'=8,'kv_1'=8,'kv_2'=2] {'kv_1'}, use_global_device_ids=true, to_apply=%region_3.4 | all-reduce | flops 2560 | bytes 20480 | tf_op jit(solution)/shard_map/pmax | solution.py:17
  187.2 3.3 pmax.170
  190.5 10.1 %fusion.8 = (f32[20,128]{1,0:T(8,128)S(1)}, f32[20,128]{1,0:T(8,128)S(1)}, f32[20,128]{1,0:T(8,128)S(1)}, f32[20,128]{1,0:T(8,128)S(1)}, f32[20,128]{1,0:T(8,128...) fusion(f32[20,128,256]{2,1,0:T(8,128)} %get-tuple-element.62, ...), kind=kOutput, calls=%fused_computation.24 | convolution fusion | flops 184135680 | bytes 23685376 | tf_op jit(solution)/shard_map/qhd,khd->hqk/dot_general | solution.py:60
  205.2 3.6 convolution_add_fusion.7
  209.0 74.2 %all-reduce.29.cloned.1.call-done = (f32[20,128]{1,0:T(8,128)}, f32[20,128]{1,0:T(8,128)}, f32[20,128]{1,0:T(8,128)}, f32[20,128]{1,0:T(8,128)}, f32[20,128]{1,0...) async-done(((f32[20,128]{1,0:T(8,128)}, f32[20,128]{1,0:T(8,128)}, f32[20,128]{1,0:T(8,128)}, f32[20,128]{1,0:T(8,128)}, f32[20,128]{1,0:T(8,128)}, ...) | async-done | bytes 71696 | tf_op jit(solution)/shard_map/pmax | solution.py:17
  283.3 77.3 %all-reduce.27.cloned.1.call-done = (f32[20,128]{1,0:T(8,128)}, f32[20,128]{1,0:T(8,128)}, f32[20,128]{1,0:T(8,128)}, f32[20,128]{1,0:T(8,128)}, f32[20,128]{1,0...) async-done(((f32[20,128]{1,0:T(8,128)}, f32[20,128]{1,0:T(8,128)}, f32[20,128]{1,0:T(8,128)}, f32[20,128]{1,0:T(8,128)}, f32[20,128]{1,0:T(8,128)}, ...) | async-done | bytes 71696 | tf_op jit(solution)/shard_map/pmax | solution.py:17
  363.2 2.9 copy.75
  371.3 24.9 %all-reduce.31.cloned.1.call-done = (f32[20,128]{1,0:T(8,128)}, f32[20,128]{1,0:T(8,128)}, f32[20,128]{1,0:T(8,128)}, f32[20,128]{1,0:T(8,128)}, f32[20,128]{1,0...) async-done(((f32[20,128]{1,0:T(8,128)}, f32[20,128]{1,0:T(8,128)}, f32[20,128]{1,0:T(8,128)}, f32[20,128]{1,0:T(8,128)}, f32[20,128]{1,0:T(8,128)}, ...) | async-done | bytes 71696 | tf_op jit(solution)/shard_map/pmax | solution.py:17
  408.2 8.6 %fusion.10 = (f32[20,128]{1,0:T(8,128)S(1)}, f32[20,128]{1,0:T(8,128)S(1)}, f32[20,128]{1,0:T(8,128)S(1)}, f32[20,128]{1,0:T(8,128)S(1)}, f32[20,128]{1,0:T(8,12...) fusion(f32[20,128,256]{2,1,0:T(8,128)} %get-tuple-element.65, f32[20,128]{1,0:T(8,128)S(1)} %copy-done.8, ...), kind=kLoop, calls=%fused_computation.26 | loop fusion | flops 18332160 | bytes 18493696 | tf_op jit(solution)/shard_map/reduce_sum | solution.py:76
  418.7 2.9 copy.82
  426.8 2.9 convolution_add_fusion.1
  439.0 2.9 convolution_add_fusion.2
  443.1 2.9 copy.80
  451.3 2.9 convolution_add_fusion.3
  455.3 2.9 copy.79
  463.5 2.9 convolution_add_fusion.4
  467.6 2.9 copy.78
  475.8 2.9 convolution_add_fusion.5
  497.0 217.5 %all-reduce.25.cloned.1.call-done = (f32[3072,128]{1,0:T(8,128)}, f32[3072,128]{1,0:T(8,128)}, f32[3072,128]{1,0:T(8,128)}, f32[3072,128]{1,0:T(8,128)}, f32[307...) async-done(((f32[3072,128]{1,0:T(8,128)}, f32[3072,128]{1,0:T(8,128)}, f32[3072,128]{1,0:T(8,128)}, f32[3072,128]{1,0:T(8,128)}, ...) | async-done | bytes 12582928
  (150 shorter events, 115.6 us)
Async XLA Ops:
  6.5 102.6 %all-gather.2.cloned.1.call-start = ((), (), s32[]{:S(2)}) async-start(), calls=%async_computation | async-start | bytes 5283840 | tf_op jit(solution)/shard_map/all_gather | solution.py:43
  7.3 275.9 %all-reduce.29.cloned.1.call-start = ((), (), s32[]{:S(2)}) async-start(), calls=%async_computation.3 | async-start | bytes 172032 | tf_op jit(solution)/shard_map/pmax | solution.py:17
  14.4 2.8 copy-start.15
  14.4 2.8 copy-start.16
  109.1 3.6 copy-start.7
  112.7 2.1 copy-start.6
  200.6 4.6 copy-start
  208.9 151.8 %all-reduce.27.cloned.1.call-start = ((), (), s32[]{:S(2)}) async-start(), calls=%async_computation.2 | async-start | bytes 172032 | tf_op jit(solution)/shard_map/pmax | solution.py:17
  283.3 112.9 %all-reduce.31.cloned.1.call-start = ((), (), s32[]{:S(2)}) async-start(), calls=%async_computation.4 | async-start | bytes 172032 | tf_op jit(solution)/shard_map/pmax | solution.py:17
  360.7 353.8 %all-reduce.25.cloned.1.call-start = ((), (), s32[]{:S(2)}) async-start(), calls=%async_computation.1 | async-start | bytes 25165824
  396.2 4.3 copy-start.12
  396.2 4.3 copy-start.13
  398.1 4.0 copy-start.11
  398.1 10.1 %copy-start.3 = (f32[20,128,256]{2,1,0:T(8,128)S(1)}, f32[20,128,256]{2,1,0:T(8,128)}, u32[]{:S(2)}) copy-start(f32[20,128,256]{2,1,0:T(8,128)} %fusion.69) | copy-start | bytes 7864324
  400.4 3.1 copy-start.10
  402.1 3.0 copy-start.9
  402.1 6.1 copy-start.2
  403.5 3.0 copy-start.8
  405.1 3.1 copy-start.1
  405.1 3.1 copy-start.14
  408.1 8.6 %copy-start.4 = (f32[20,128,256]{2,1,0:T(8,128)S(1)}, f32[20,128,256]{2,1,0:T(8,128)}, u32[]{:S(2)}) copy-start(f32[20,128,256]{2,1,0:T(8,128)} %fusion.70) | copy-start | bytes 7864324
  485.4 2.7 copy-start.5
  495.0 0.7 copy-start.17
Sparse Core Ops, SparseCore 0:
  9.9 99.1 all-gather.1
  209.0 74.1 all-reduce.28
  286.1 74.4 all-reduce.26
  363.6 32.5 all-reduce.30
  495.2 219.2 all-reduce.24
where the time goes:
time: 736 us; the launch traced here: 734 us
  waiting for transfers between devices  482 us (65%)
  local copies, waits for them, and re-layouts  85.4 us (12%)
  matrix products  61.6 us (8%)
  blocking collectives  58.7 us (8%)
  other arithmetic  30.5 us (4%)
  between operations  14.8 us (2%)
    unnamed x6, waiting for transfers between devices  218 us
    pmax x3, waiting for transfers between devices, by_axis(): return functools.reduce(lax.pmax, axes, x)  176 us
    all_gather x1, waiting for transfers between devices, per_device(): gathered = lax.all_gather(queries, KV, axis=0, tiled=True)  87.6 us
    pmax x3, blocking collectives, by_axis(): return functools.reduce(lax.pmax, axes, x)  58.7 us
    unnamed x47, local copies, waits for them, and re-layouts  27.6 us
    dot_general x8, matrix products, per_device(): jnp.einsum('qhd,khd->hqk', sub_block, ckeys, preferred_element_type=jnp.f...  25 us
    dot_general x8, matrix products, per_device(): jnp.einsum('hqk,khd->qhd', cache_weight.astype(jnp.bfloat16), cache_value...  21.2 us
    pad x8, local copies, waits for them, and re-layouts, sum_packed(): jnp.pad(lines, ((0, 0), (0, extent * 128 - lines.shape[1])))  20.2 us
  transfers between devices with their start and end apart: 5, of which 5 were waited for; matrix products, arithmetic and copies ran while one was open for 3% of the time, Pallas kernels for 0%

commit v1 on v0

--- a/solution.py
+++ b/solution.py
@@ -40,7 +40,9 @@
     q_dev, heads, head_dim = queries.shape
     cache_dev = cache_keys.shape[0]
     factor = 1.0 / math.sqrt(head_dim)
-    gathered = lax.all_gather(queries, KV, axis=0, tiled=True)
+    gathered = jnp.concatenate(
+        lax.all_to_all(jnp.stack([queries] * lax.axis_size(KV)), KV, 0, 0), axis=0
+    )
     devices = lax.axis_size(KV)
     position = lax.axis_index(KV) * cache_dev + lax.iota(jnp.int32, cache_dev)
     live = position < valid_frames[0] * FRAME

time: 736 us -> 822 us (1.12)
  waiting for transfers between devices: 482 us -> 519 us
  starting transfers between devices: 0.25 us -> 27.7 us
  blocking collectives: 58.7 us -> 75.3 us
    all_to_all x0 -> x1, waiting for transfers between devices: none -> 110 us  [per_device(): lax.all_to_all(jnp.stack([queries] * lax.axis_size(KV)), KV, 0, 0)]
    all_gather x1 -> x0, waiting for transfers between devices: 87.6 us -> none  [per_device(): gathered = lax.all_gather(queries, KV, axis=0, tiled=True)]
    all_to_all x0 -> x1, starting transfers between devices: none -> 27.1 us  [per_device(): lax.all_to_all(jnp.stack([queries] * lax.axis_size(KV)), KV, 0, 0)]
    pmax x3, blocking collectives: 58.7 us -> 75.3 us  [by_axis(): return functools.reduce(lax.pmax, axes, x)]
    pmax x3, waiting for transfers between devices: 176 us -> 192 us  [by_axis(): return functools.reduce(lax.pmax, axes, x)]
    unnamed x6 -> x5, waiting for transfers between devices: 218 us -> 218 us
    unnamed x47 -> x49, local copies, waits for them, and re-layouts: 27.6 us -> 26.9 us
where the time goes in v1:
time: 822 us; the launch traced here: 816 us
  waiting for transfers between devices  519 us (63%)
  local copies, waits for them, and re-layouts  87.6 us (11%)
  blocking collectives  75.3 us (9%)
  matrix products  60.8 us (7%)
  other arithmetic  30.5 us (4%)
  starting transfers between devices  27.7 us (3%)
  between operations  15.2 us (2%)
    unnamed x5, waiting for transfers between devices  218 us
    pmax x3, waiting for transfers between devices, by_axis(): return functools.reduce(lax.pmax, axes, x)  192 us
    all_to_all x1, waiting for transfers between devices, per_device(): lax.all_to_all(jnp.stack([queries] * lax.axis_size(KV)), KV, 0, 0)  110 us
    pmax x3, blocking collectives, by_axis(): return functools.reduce(lax.pmax, axes, x)  75.3 us
    all_to_all x1, starting transfers between devices, per_device(): lax.all_to_all(jnp.stack([queries] * lax.axis_size(KV)), KV, 0, 0)  27.1 us
    unnamed x49, local copies, waits for them, and re-layouts  26.9 us
    dot_general x8, matrix products, per_device(): jnp.einsum('qhd,khd->hqk', sub_block, ckeys, preferred_element_type=jnp.f...  24.8 us
    dot_general x8, matrix products, per_device(): jnp.einsum('hqk,khd->qhd', cache_weight.astype(jnp.bfloat16), cache_value...  21.2 us
  transfers between devices with their start and end apart: 5, of which 5 were waited for; matrix products, arithmetic and copies ran while one was open for 3% of the time, Pallas kernels for 0%

profile of v1, /device:TPU:518, one launch (start us, length us, event | category | flops | bytes accessed | tf_op | source)
XLA Modules:
  0.0 816.5 jit_solution(18286239357051047641)
XLA Ops:
  6.5 3.8 stack.2
  10.4 27.1 %all-to-all-start = ((bf16[128,4,40,128]{3,2,1,0:T(8,128)(2,1)}), bf16[128,4,40,128]{3,2,1,0:T(8,128)(2,1)}, u32[]{:S(2)}, u32[]{:S(2)}) async-start(bf16[128,4,40,128]{3,2,1,0:T(8,128)(2,1)} %stack.2), calls=%async_computation | async-start | bytes 10485760 | tf_op jit(solution)/shard_map/all_to_all | solution.py:44
  45.3 4.3 fusion.169
  49.6 109.9 %all-to-all-done = bf16[128,4,40,128]{3,2,1,0:T(8,128)(2,1)} async-done(((bf16[128,4,40,128]{3,2,1,0:T(8,128)(2,1)}), bf16[128,4,40,128]{3,2,1,0:T(8,128)(2,1)}, u32[]{:S(2)}, u32[]{:S(2)}) %all-to-all-start) | async-done | bytes 5242912 | tf_op jit(solution)/shard_map/all_to_all | solution.py:44
  159.5 4.6 copy.125
  182.4 33.6 %pmax.168 = f32[20,128]{1,0:T(8,128)S(1)} all-reduce(f32[20,128]{1,0:T(8,128)S(1)} %max.72), channel_id=1, replica_groups=mesh['grp'=2,'kv_0'=8,'kv_1'=8,'kv_2'=2] {'kv_0'}, use_global_device_ids=true, to_apply=%region_2.3 | all-reduce | flops 2560 | bytes 20480 | tf_op jit(solution)/shard_map/pmax | solution.py:17
  216.0 26.6 %pmax.169 = f32[20,128]{1,0:T(8,128)S(1)} all-reduce(f32[20,128]{1,0:T(8,128)S(1)} %pmax.168), channel_id=1, replica_groups=mesh['grp'=2,'kv_0'=8,'kv_1'=8,'kv_2'=2] {'kv_1'}, use_global_device_ids=true, to_apply=%region_3.4 | all-reduce | flops 2560 | bytes 20480 | tf_op jit(solution)/shard_map/pmax | solution.py:17
  242.7 15.0 %pmax.170 = f32[20,128]{1,0:T(8,128)S(1)} all-reduce(f32[20,128]{1,0:T(8,128)S(1)} %pmax.169), channel_id=1, replica_groups=mesh['grp'=2,'kv_0'=8,'kv_1'=8,'kv_2'=2] {'kv_2'}, use_global_device_ids=true, to_apply=%region_4.5 | all-reduce | flops 2560 | bytes 20480 | tf_op jit(solution)/shard_map/pmax | solution.py:17
  257.7 10.3 %fusion.8 = (f32[20,128]{1,0:T(8,128)S(1)}, f32[20,128]{1,0:T(8,128)S(1)}, f32[20,128]{1,0:T(8,128)S(1)}, f32[20,128]{1,0:T(8,128)S(1)}, f32[20,128]{1,0:T(8,128...) fusion(f32[20,128,256]{2,1,0:T(8,128)} %get-tuple-element.58, ...), kind=kOutput, calls=%fused_computation.25 | convolution fusion | flops 184135680 | bytes 23947520 | tf_op jit(solution)/shard_map/qhd,khd->hqk/dot_general | solution.py:62
  272.6 3.6 convolution_add_fusion.7
  276.3 89.4 %all-reduce.29.cloned.1.call-done = (f32[20,128]{1,0:T(8,128)}, f32[20,128]{1,0:T(8,128)}, f32[20,128]{1,0:T(8,128)}, f32[20,128]{1,0:T(8,128)}, f32[20,128]{1,0...) async-done(((f32[20,128]{1,0:T(8,128)}, f32[20,128]{1,0:T(8,128)}, f32[20,128]{1,0:T(8,128)}, f32[20,128]{1,0:T(8,128)}, f32[20,128]{1,0:T(8,128)}, ...) | async-done | bytes 71696 | tf_op jit(solution)/shard_map/pmax | solution.py:17
  365.9 77.3 %all-reduce.27.cloned.1.call-done = (f32[20,128]{1,0:T(8,128)}, f32[20,128]{1,0:T(8,128)}, f32[20,128]{1,0:T(8,128)}, f32[20,128]{1,0:T(8,128)}, f32[20,128]{1,0...) async-done(((f32[20,128]{1,0:T(8,128)}, f32[20,128]{1,0:T(8,128)}, f32[20,128]{1,0:T(8,128)}, f32[20,128]{1,0:T(8,128)}, f32[20,128]{1,0:T(8,128)}, ...) | async-done | bytes 71696 | tf_op jit(solution)/shard_map/pmax | solution.py:17
  453.8 25.0 %all-reduce.31.cloned.1.call-done = (f32[20,128]{1,0:T(8,128)}, f32[20,128]{1,0:T(8,128)}, f32[20,128]{1,0:T(8,128)}, f32[20,128]{1,0:T(8,128)}, f32[20,128]{1,0...) async-done(((f32[20,128]{1,0:T(8,128)}, f32[20,128]{1,0:T(8,128)}, f32[20,128]{1,0:T(8,128)}, f32[20,128]{1,0:T(8,128)}, f32[20,128]{1,0:T(8,128)}, ...) | async-done | bytes 71696 | tf_op jit(solution)/shard_map/pmax | solution.py:17
  490.8 8.7 %fusion.10 = (f32[20,128]{1,0:T(8,128)S(1)}, f32[20,128]{1,0:T(8,128)S(1)}, f32[20,128]{1,0:T(8,128)S(1)}, f32[20,128]{1,0:T(8,128)S(1)}, f32[20,128]{1,0:T(8,12...) fusion(f32[20,128,256]{2,1,0:T(8,128)} %get-tuple-element.61, f32[20,128]{1,0:T(8,128)S(1)} %copy-done.9, ...), kind=kLoop, calls=%fused_computation.27 | loop fusion | flops 18332160 | bytes 18493696 | tf_op jit(solution)/shard_map/reduce_sum | solution.py:78
  509.5 2.9 convolution_add_fusion.1
  513.5 2.9 copy.54
  521.6 2.9 convolution_add_fusion.2
  533.7 2.9 convolution_add_fusion.3
  537.8 2.9 copy.52
  545.9 2.9 convolution_add_fusion.4
  550.0 2.9 copy.51
  558.1 2.9 convolution_add_fusion.5
  562.1 2.9 copy.50
  579.5 217.5 %all-reduce.25.cloned.1.call-done = (f32[3072,128]{1,0:T(8,128)}, f32[3072,128]{1,0:T(8,128)}, f32[3072,128]{1,0:T(8,128)}, f32[3072,128]{1,0:T(8,128)}, f32[307...) async-done(((f32[3072,128]{1,0:T(8,128)}, f32[3072,128]{1,0:T(8,128)}, f32[3072,128]{1,0:T(8,128)}, f32[3072,128]{1,0:T(8,128)}, ...) | async-done | bytes 12582928
  (152 shorter events, 118.8 us)
Async XLA Ops:
  10.3 28.2 %copy-start.6 = (bf16[256,40,128]{2,1,0:T(8,128)(2,1)S(1)}, bf16[256,40,128]{2,1,0:T(8,128)(2,1)}, u32[]{:S(2)}) copy-start(bf16[256,40,128]{2,1,0:T(8,128)(2,1)} %param.8) | copy-start | bytes 7864324
  10.4 149.1 %all-to-all-start = ((bf16[128,4,40,128]{3,2,1,0:T(8,128)(2,1)}), bf16[128,4,40,128]{3,2,1,0:T(8,128)(2,1)}, u32[]{:S(2)}, u32[]{:S(2)}) async-start(bf16[128,4,40,128]{3,2,1,0:T(8,128)(2,1)} %stack.2), calls=%async_computation | async-start | bytes 10485760 | tf_op jit(solution)/shard_map/all_to_all | solution.py:44
  37.4 328.3 %all-reduce.29.cloned.1.call-start = ((), (), s32[]{:S(2)}) async-start(), calls=%async_computation.3 | async-start | bytes 172032 | tf_op jit(solution)/shard_map/pmax | solution.py:17
  43.1 2.1 copy-start.16
  43.1 2.1 copy-start.17
  159.5 4.6 copy-start.8
  164.1 16.1 %copy-start = (bf16[128,4,40,128]{3,0,2,1:T(8,128)(2,1)}, bf16[128,4,40,128]{3,0,2,1:T(8,128)(2,1)S(1)}, u32[]{:S(2)}) copy-start(bf16[128,4,40,128]{3,0,2,1:T(8,128)(2,1)S(1)} %copy.125) | copy-start | bytes 15728644
  166.5 2.0 copy-start.7
  276.2 167.0 %all-reduce.27.cloned.1.call-start = ((), (), s32[]{:S(2)}) async-start(), calls=%async_computation.2 | async-start | bytes 172032 | tf_op jit(solution)/shard_map/pmax | solution.py:17
  365.8 113.1 %all-reduce.31.cloned.1.call-start = ((), (), s32[]{:S(2)}) async-start(), calls=%async_computation.4 | async-start | bytes 172032 | tf_op jit(solution)/shard_map/pmax | solution.py:17
  443.2 353.7 %all-reduce.25.cloned.1.call-start = ((), (), s32[]{:S(2)}) async-start(), calls=%async_computation.1 | async-start | bytes 25165824
  478.9 4.2 copy-start.13
  478.9 4.2 copy-start.14
  480.8 3.9 copy-start.12
  480.8 10.0 %copy-start.3 = (f32[20,128,256]{2,1,0:T(8,128)S(1)}, f32[20,128,256]{2,1,0:T(8,128)}, u32[]{:S(2)}) copy-start(f32[20,128,256]{2,1,0:T(8,128)} %fusion.69) | copy-start | bytes 7864324
  483.1 3.1 copy-start.11
  484.7 3.0 copy-start.10
  484.7 6.1 copy-start.2
  486.1 3.1 copy-start.9
  487.7 3.1 copy-start.1
  487.7 3.1 copy-start.15
  490.8 8.7 %copy-start.4 = (f32[20,128,256]{2,1,0:T(8,128)S(1)}, f32[20,128,256]{2,1,0:T(8,128)}, u32[]{:S(2)}) copy-start(f32[20,128,256]{2,1,0:T(8,128)} %fusion.70) | copy-start | bytes 7864324
  567.7 2.7 copy-start.5
  577.6 0.7 copy-start.18
Sparse Core Ops, SparseCore 0:
  276.3 89.3 all-reduce.28
  368.6 74.4 all-reduce.26
  446.3 32.5 all-reduce.30
  577.7 219.1 all-reduce.24
